TPU v7x, 256 devices: a whole 4x4x8 slice. The times are simulated.
256 devices in a mesh: dp: 8 (over z), expert: 32 (over x, y, core).
Axes of the slice: x: 4, y: 4, z: 8, core: 2. Of those that a mesh axis runs over, the one named last changes fastest.
Arguments:
- tokens: bfloat16 [65536, 2048], P(('dp', 'expert')), may hold values from -6 to 6
- expert_ranks: int32 [32, 65536], P(None, ('dp', 'expert')), may hold values from 0 to 65535, as said below
- capacity: int32 [32], replicated, may hold values from 512 to 1024, as said below
- weight_in: bfloat16 [32, 2048, 8192], P('expert', None, 'dp'), may hold values from -0.125 to 0.125
- weight_out: bfloat16 [32, 8192, 2048], P('expert', 'dp'), may hold values from -0.0625 to 0.0625
- gate_weights: float32 [32, 1024], P('expert', 'dp'), may hold values from 0.05 to 1
Outputs:
- combined: bfloat16 [65536, 2048], P(('dp', 'expert'))
Inputs may be any that keep to these rules, and one draw needn't show every extreme that they name: `expert_ranks`: for each expert the ranks are a permutation of 0 to 65535. Of the 256 tokens of one device, at most 8 have rank under 1024 for one expert; for an expert of capacity 1024, some devices have exactly 8. At least one expert has capacity 1024.
All inputs are finite; a program needn't handle non-finite values.
Results may differ from a plain program's by a relative error of at most 0.0053.
Values may be sent and summed in bfloat16 or wider, within the bound.
No kernel may reach another device: no remote copies, remote signals or barrier semaphores. Data moves between devices by JAX's collectives and lax.ppermute only.
A program may use at most 64 MiB of HBM per device.

v0:
```python
import jax
import jax.numpy as jnp
from jax import lax
from jax.sharding import Mesh
from jax.sharding import PartitionSpec as P

MOST = 8
LANES = 128
EXPERT = ("expert_0", "expert_1", "expert_2")
DP_EXPERT = ("dp", "expert_0", "expert_1", "expert_2")


def exclusive(values):
    return jnp.cumsum(values) - values


def on_device(tokens, expert_ranks, capacity, weight_in, weight_out, gate_weights):
    dp_count = lax.axis_size("dp")
    expert_count = lax.axis_size(EXPERT)
    token_count, width = tokens.shape
    slots_dp = gate_weights.shape[1]
    rows_all = expert_count * MOST
    own_dp = lax.axis_index("dp")
    own_expert = lax.axis_index(EXPERT)
    chosen = expert_ranks < capacity[:, None]
    chosen_int = chosen.astype(jnp.int32)
    counts = jnp.sum(chosen_int, axis=1)
    before = jnp.cumsum(chosen_int, axis=1) - chosen_int
    places = lax.broadcasted_iota(jnp.int32, (expert_count, MOST, token_count), 1)
    pack_table = jnp.logical_and(chosen[:, None, :], before[:, None, :] == places)
    pack_table = pack_table.astype(jnp.bfloat16).reshape(rows_all, token_count)
    packed = jnp.dot(pack_table, tokens, preferred_element_type=jnp.float32).astype(jnp.bfloat16)
    arrived_rows = lax.all_to_all(
        packed.reshape(expert_count, MOST, width), EXPERT, split_axis=0, concat_axis=0, tiled=True
    ).reshape(rows_all, width)
    device_ids = lax.broadcasted_iota(jnp.int32, (expert_count, expert_count), 0)
    expert_ids = lax.broadcasted_iota(jnp.int32, (expert_count, expert_count), 1)
    table = jnp.where(device_ids == own_expert, counts[None, :], 0)
    table = lax.psum(table.reshape(-1, LANES), EXPERT).reshape(expert_count, expert_count)
    arrived = jnp.sum(jnp.where(expert_ids == own_expert, table, 0), axis=1)
    plane_ids = lax.broadcasted_iota(jnp.int32, (dp_count, LANES), 0)
    lane_ids = lax.broadcasted_iota(jnp.int32, (dp_count, LANES), 1)
    plane_row = jnp.pad(jnp.sum(table, axis=0).astype(jnp.float32), (0, LANES - expert_count))
    both = jnp.concatenate(
        [
            jnp.where(plane_ids == own_dp, plane_row[None, :], 0.0),
            jnp.where(plane_ids == own_dp, gate_weights.reshape(-1, LANES), 0.0),
        ]
    )
    both = lax.psum(both, "dp")
    plane_counts = both[:dp_count].astype(jnp.int32)
    most_rows = jnp.max(plane_counts)
    earlier = jnp.logical_and(plane_ids < own_dp, lane_ids == own_expert)
    first_slot = jnp.sum(jnp.where(earlier, plane_counts, 0))
    gates_all = jnp.concatenate([both[dp_count:].reshape(-1), jnp.zeros((rows_all,), jnp.float32)])
    within = lax.broadcasted_iota(jnp.int32, (expert_count, MOST), 1)
    target = jnp.where(within < arrived[:, None], exclusive(arrived)[:, None] + within, -1).reshape(
        rows_all
    )

    def experts(rows, plane_rows):
        slot_ids = lax.broadcasted_iota(jnp.int32, (rows_all, plane_rows), 1)
        place_table = (target[:, None] == slot_ids).astype(jnp.bfloat16)
        plane = lax.dot_general(
            place_table, rows, (((0,), (0,)), ((), ())), preferred_element_type=jnp.float32
        ).astype(jnp.bfloat16)
        slot_rows = lax.all_gather(plane, "dp", axis=0, tiled=True)
        hidden = jnp.maximum(
            jnp.dot(slot_rows, weight_in[0], preferred_element_type=jnp.float32), 0.0
        ).astype(jnp.bfloat16)
        share = jnp.dot(hidden, weight_out[0], preferred_element_type=jnp.float32)
        out = lax.psum_scatter(
            share.astype(jnp.bfloat16), "dp", scatter_dimension=0, tiled=True
        ).astype(jnp.float32)
        gates = lax.dynamic_slice_in_dim(gates_all, first_slot, plane_rows, 0)
        scaled = (gates[:, None] * out).astype(jnp.bfloat16)
        returned = jnp.dot(place_table, scaled, preferred_element_type=jnp.float32)
        return returned.astype(jnp.bfloat16)

    fair = slots_dp + slots_dp // 4
    sent_back = lax.cond(
        most_rows <= fair,
        lambda rows: experts(rows, fair),
        lambda rows: experts(rows, rows_all),
        arrived_rows,
    )
    results = lax.all_to_all(
        sent_back.reshape(expert_count, MOST, width),
        EXPERT,
        split_axis=0,
        concat_axis=0,
        tiled=True,
    ).reshape(rows_all, width)
    combined = lax.dot_general(
        pack_table, results, (((0,), (0,)), ((), ())), preferred_element_type=jnp.float32
    )
    return combined.astype(jnp.bfloat16)


def solution(mesh):
    split = Mesh(
        mesh.devices.reshape(mesh.shape["dp"], 4, 4, 2), ("dp", "expert_0", "expert_1", "expert_2")
    )
    placed = (
        P(DP_EXPERT, None),
        P(None, DP_EXPERT),
        P(),
        P(EXPERT, None, "dp"),
        P(EXPERT, "dp", None),
        P(EXPERT, "dp"),
    )
    return jax.shard_map(
        on_device, mesh=split, in_specs=placed, out_specs=P(DP_EXPERT, None), check_vma=False
    )
```

profile of v0, /device:TPU:1, one launch (start us, length us, event | category | flops | bytes accessed | tf_op | source)
XLA Modules:
  0.0 348.8 jit_solution(17893966849262882347)
XLA Ops:
  6.5 0.9 convert_bitcast_fusion.1
  7.5 0.6 reduce-window.18
  8.1 0.2 slice_reduce_fusion
  8.3 0.1 iota.90
  8.4 0.1 convert_subtract_fusion
  8.5 1.5 fusion.19
  10.0 8.6 %all-to-all-start = ((bf16[32,8,2048]{2,1,0:T(8,128)(2,1)}), bf16[32,8,2048]{2,1,0:T(8,128)(2,1)S(1)}, u32[]{:S(2)}, u32[]{:S(2)}) async-start(bf16[32,8,2048]{2,1,0:T(8,128)(2,1)} %fusion.19), calls=%async_computation.2 | async-start | bytes 2097152 | tf_op jit(solution)/shard_map/all_to_all | solution.py:33
  18.6 0.1 iota.79
  18.7 0.1 iota.80
  18.8 0.1 broadcast_in_dim.57
  18.9 0.1 reshape.73
  18.9 127.0 %psum.14 = s32[32,32]{1,0:T(8,128)S(1)} all-reduce(s32[32,32]{1,0:T(8,128)S(1)} %reshape.73), channel_id=1, replica_groups=mesh['dp'=8,'expert_0'=4,'expert_1'=4,'expert_2'=2] {'expert_0','expert_..., use_global_device_ids=true, to_apply=%region_3.4 | all-reduce | flops 1024 | bytes 8192 | tf_op jit(solution)/shard_map/psum | solution.py:39
  145.9 0.1 select_reduce_fusion
  146.1 0.1 broadcast_select_fusion.1
  146.1 16.5 %psum.15 = f32[16,128]{1,0:T(8,128)S(1)} all-reduce(f32[16,128]{1,0:T(8,128)S(1)} %pad_maximum_fusion), channel_id=1, replica_groups=mesh['dp'=8,'expert_0'=4,'expert_1'=4,'expert_2'=2] {'dp'}, use_global_device_ids=true, to_apply=%region_5.6 | all-reduce | flops 2048 | bytes 16384 | tf_op jit(solution)/shard_map/psum | solution.py:50
  162.7 0.8 select_reduce_fusion.1
  164.2 0.1 copy.19
  164.2 0.1 reduce-window.20
  164.3 0.1 reduce.1
  164.4 0.1 add_select_fusion
  164.5 151.7 %conditional.2 = (bf16[256,2048]{1,0:T(8,128)(2,1)S(1)}) conditional(s32[]{:T(128)} %convert_element_type.61, (s32[32,8]{1,0:T(8,128)S(1)}, s32[]{:T(128)}, f32[1280]{0:T(1024)S(1)}, bf16[256,2048]{1,0:T(8,128)(2,1)S(1)}, bf16[1,2048,1024]{2,1,0:T(8,128)(2,1)}, /*index=5*/bf16[1,1024,2048]{2,1,0:T(8,128)(2,1)}) %tuple.30, (s32[32,8]{1,0:T(8,128)S(1)}, ...), branch_computations={%region_10.12_spmd, %region_12.14_spmd} | conditional | flops 17727356928 | bytes 85990520
  164.5 0.0 all-gather.5.cloned.1.call-start
  164.6 0.1 eq.49
  164.7 1.3 convolution_convert_fusion.3
  166.0 0.2 reduce-scatter.5.cloned.1.call-start
  166.2 67.1 %all-gather.5.cloned.1.call-done = bf16[1280,2048]{1,0:T(8,128)(2,1)} async-done(((bf16[160,2048]{1,0:T(8,128)(2,1)}), bf16[1280,2048]{1,0:T(8,128)(2,1)}) %all-gather.5.cloned.1.call-update) | async-done | bytes 5242896 | tf_op jit(solution)/shard_map/cond/branch_1_fun/all_gather | solution.py:67
  233.4 16.9 %convolution_convert_fusion.2 = bf16[1280,2048]{1,0:T(8,128)(2,1)} fusion(bf16[1,1024,2048]{2,1,0:T(8,128)(2,1)} %get-tuple-element.45, bf16[1280,2048]{1,0:T(8,128)(2,1)} %all-gather.5.cloned.1.call-done, bf16[1,2048,1024]{2,1,0:T(8,128)(2,1)} %get-tuple-element.44), kind=kOutput, calls=%fused_computation.13 | convolution fusion | flops 10742661120 | bytes 18874368 | tf_op jit(solution)/shard_map/cond/branch_1_fun/dot_general | solution.py:71
  252.0 0.1 dynamic_slice.5
  252.0 62.3 %reduce-scatter.5.cloned.1.call-done = bf16[160,2048]{1,0:T(8,128)(2,1)} async-done(((bf16[1280,2048]{1,0:T(8,128)(2,1)}), bf16[160,2048]{1,0:T(8,128)(2,1)}) %reduce-scatter.5.cloned.1.call-update) | async-done | bytes 655376 | tf_op jit(solution)/shard_map/cond/branch_1_fun/reduce_scatter | solution.py:72
  314.4 1.6 fusion.13
  316.2 24.3 %all_to_all.10 = bf16[32,8,2048]{2,1,0:T(8,128)(2,1)S(1)} all-to-all(bf16[32,8,2048]{2,1,0:T(8,128)(2,1)S(1)} %bitcast.57), channel_id=1, replica_groups=mesh['dp'=8,'expert_0'=4,'expert_1'=4,'expert_2'=2] {'expert_0','expert_..., dimensions={0} | all-to-all | bytes 2097152 | tf_op jit(solution)/shard_map/all_to_all | solution.py:87
  340.5 1.5 fusion.18
  (24 shorter events, 0.2 us)
Async XLA Ops:
  6.5 2.0 copy-start
  6.5 139.5 %copy-start.1 = (f32[1,128]{1,0:T(1,128)S(1)}, f32[1,128]{1,0:T(1,128)}, u32[]{:S(2)}) copy-start(f32[1,128]{1,0:T(1,128)} %param.13) | copy-start | bytes 1540
  10.0 154.5 %all-to-all-start = ((bf16[32,8,2048]{2,1,0:T(8,128)(2,1)}), bf16[32,8,2048]{2,1,0:T(8,128)(2,1)S(1)}, u32[]{:S(2)}, u32[]{:S(2)}) async-start(bf16[32,8,2048]{2,1,0:T(8,128)(2,1)} %fusion.19), calls=%async_computation.2 | async-start | bytes 2097152 | tf_op jit(solution)/shard_map/all_to_all | solution.py:33
  164.5 68.8 %all-gather.5.cloned.1.call-start = ((), (), s32[]{:S(2)}) async-start(), calls=%async_computation.6 | async-start | bytes 5898240 | tf_op jit(solution)/shard_map/cond/branch_1_fun/all_gather | solution.py:67
  166.0 148.4 %reduce-scatter.5.cloned.1.call-start = ((), (), s32[]{:S(2)}) async-start(), calls=%async_computation.7 | async-start | bytes 5898240 | tf_op jit(solution)/shard_map/cond/branch_1_fun/reduce_scatter | solution.py:72
Sparse Core Ops, SparseCore 0:
  167.1 66.1 all-gather.4
  250.4 63.9 reduce-scatter.4
where the time goes:
time: 349 us
  blocking collectives  168 us (48%)
  waiting for transfers between devices  129 us (37%)
  matrix products  22.7 us (7%)
  between operations  14.2 us (4%)
  starting transfers between devices  8.84 us (3%)
    psum x1, blocking collectives, on_device(): lax.psum(table.reshape(-1, LANES), EXPERT)  127 us
    all_gather x1, waiting for transfers between devices, experts(): slot_rows = lax.all_gather(plane, 'dp', axis=0, tiled=True)  67.1 us
    reduce_scatter x1, waiting for transfers between devices, experts(): lax.psum_scatter(share.astype(jnp.bfloat16), 'dp', scatter_dimension=0, t...  62.3 us
    all_to_all x1, blocking collectives, on_device(): lax.all_to_all(sent_back.reshape(expert_count, MOST, width), EXPERT, spli...  24.3 us
    dot_general x1, matrix products, experts(): share = jnp.dot(hidden, weight_out[0], preferred_element_type=jnp.float32)  16.9 us
    psum x1, blocking collectives, on_device(): both = lax.psum(both, 'dp')  16.5 us
    all_to_all x1, starting transfers between devices, on_device(): lax.all_to_all(packed.reshape(expert_count, MOST, width), EXPERT, split_a...  8.58 us
  transfers between devices with their start and end apart: 3, of which 2 were waited for; matrix products, arithmetic and copies ran while one was open for 1% of the time, Pallas kernels for 0%

commit v1 on v0

--- a/solution.py
+++ b/solution.py
@@ -36,7 +36,15 @@
     device_ids = lax.broadcasted_iota(jnp.int32, (expert_count, expert_count), 0)
     expert_ids = lax.broadcasted_iota(jnp.int32, (expert_count, expert_count), 1)
     table = jnp.where(device_ids == own_expert, counts[None, :], 0)
-    table = lax.psum(table.reshape(-1, LANES), EXPERT).reshape(expert_count, expert_count)
+
+    def tiles_carry(inp):
+        axis_id = "expert_0"
+        axis_tag = ("expert_1", "expert_2")
+        for to_i in (axis_tag, axis_id):
+            inp = lax.psum(inp, to_i)
+        return inp
+
+    table = tiles_carry(table.reshape(-1, LANES)).reshape(expert_count, expert_count)
     arrived = jnp.sum(jnp.where(expert_ids == own_expert, table, 0), axis=1)
     plane_ids = lax.broadcasted_iota(jnp.int32, (dp_count, LANES), 0)
     lane_ids = lax.broadcasted_iota(jnp.int32, (dp_count, LANES), 1)

time: 349 us -> 252 us (0.72)
  blocking collectives: 168 us -> 70.6 us
    psum x1 -> x2, blocking collectives: 127 us -> 29.8 us  [tiles_carry(): inp = lax.psum(inp, to_i)]
where the time goes in v1:
time: 252 us
  waiting for transfers between devices  130 us (52%)
  blocking collectives  70.6 us (28%)
  matrix products  22.7 us (9%)
  between operations  14.2 us (6%)
  starting transfers between devices  8.84 us (4%)
  other arithmetic  2.95 us (1%)
    all_gather x1, waiting for transfers between devices, experts(): slot_rows = lax.all_gather(plane, 'dp', axis=0, tiled=True)  67.2 us
    reduce_scatter x1, waiting for transfers between devices, experts(): lax.psum_scatter(share.astype(jnp.bfloat16), 'dp', scatter_dimension=0, t...  62.3 us
    psum x2, blocking collectives, tiles_carry(): inp = lax.psum(inp, to_i)  29.8 us
    all_to_all x1, blocking collectives, on_device(): lax.all_to_all(sent_back.reshape(expert_count, MOST, width), EXPERT, spli...  24.3 us
    dot_general x1, matrix products, experts(): share = jnp.dot(hidden, weight_out[0], preferred_element_type=jnp.float32)  16.9 us
    psum x1, blocking collectives, on_device(): both = lax.psum(both, 'dp')  16.5 us
    all_to_all x1, starting transfers between devices, on_device(): lax.all_to_all(packed.reshape(expert_count, MOST, width), EXPERT, split_a...  8.58 us
  transfers between devices with their start and end apart: 3, of which 2 were waited for; matrix products, arithmetic and copies ran while one was open for 1% of the time, Pallas kernels for 0%

profile of v1, /device:TPU:1, one launch (start us, length us, event | category | flops | bytes accessed | tf_op | source)
XLA Modules:
  0.0 251.7 jit_solution(13561348546763715642)
XLA Ops:
  6.5 0.9 convert_bitcast_fusion.1
  7.5 0.6 reduce-window.18
  8.1 0.2 slice_reduce_fusion
  8.3 0.1 iota.90
  8.4 0.1 convert_subtract_fusion
  8.5 1.5 fusion.19
  10.0 8.6 %all-to-all-start = ((bf16[32,8,2048]{2,1,0:T(8,128)(2,1)}), bf16[32,8,2048]{2,1,0:T(8,128)(2,1)S(1)}, u32[]{:S(2)}, u32[]{:S(2)}) async-start(bf16[32,8,2048]{2,1,0:T(8,128)(2,1)} %fusion.19), calls=%async_computation.2 | async-start | bytes 2097152 | tf_op jit(solution)/shard_map/all_to_all | solution.py:33
  18.6 0.1 iota.79
  18.7 0.1 iota.80
  18.8 0.1 broadcast_in_dim.57
  18.9 11.6 %psum.21 = s32[8,128]{1,0:T(8,128)S(1)} all-reduce(s32[8,128]{1,0:T(8,128)S(1)} %broadcast_select_fusion.2), channel_id=1, replica_groups=mesh['dp'=8,'expert_0'=4,'expert_1'=4,'expert_2'=2] {'expert_1','expert_2'}, use_global_device_ids=true, to_apply=%region_3.4 | all-reduce | flops 1024 | bytes 8192 | tf_op jit(solution)/shard_map/psum | solution.py:44
  30.5 0.1 reshape.73
  30.5 18.2 %psum.22 = s32[32,32]{1,0:T(8,128)S(1)} all-reduce(s32[32,32]{1,0:T(8,128)S(1)} %reshape.73), channel_id=1, replica_groups=mesh['dp'=8,'expert_0'=4,'expert_1'=4,'expert_2'=2] {'expert_0'}, use_global_device_ids=true, to_apply=%region_4.5 | all-reduce | flops 1024 | bytes 8192 | tf_op jit(solution)/shard_map/psum | solution.py:44
  48.7 0.1 select_reduce_fusion
  48.9 0.1 broadcast_select_fusion.1
  49.0 16.5 %psum.23 = f32[16,128]{1,0:T(8,128)S(1)} all-reduce(f32[16,128]{1,0:T(8,128)S(1)} %pad_maximum_fusion), channel_id=1, replica_groups=mesh['dp'=8,'expert_0'=4,'expert_1'=4,'expert_2'=2] {'dp'}, use_global_device_ids=true, to_apply=%region_6.7 | all-reduce | flops 2048 | bytes 16384 | tf_op jit(solution)/shard_map/psum | solution.py:58
  65.5 0.8 select_reduce_fusion.1
  67.0 0.1 copy.19
  67.1 0.1 reduce-window.20
  67.1 0.1 reduce.1
  67.3 0.1 add_select_fusion
  67.4 151.8 %conditional.2 = (bf16[256,2048]{1,0:T(8,128)(2,1)S(1)}) conditional(s32[]{:T(128)} %convert_element_type.61, (s32[32,8]{1,0:T(8,128)S(1)}, s32[]{:T(128)}, f32[1280]{0:T(1024)S(1)}, bf16[256,2048]{1,0:T(8,128)(2,1)S(1)}, bf16[1,2048,1024]{2,1,0:T(8,128)(2,1)}, /*index=5*/bf16[1,1024,2048]{2,1,0:T(8,128)(2,1)}) %tuple.30, (s32[32,8]{1,0:T(8,128)S(1)}, ...), branch_computations={%region_11.13_spmd, %region_13.15_spmd} | conditional | flops 17727356928 | bytes 85990520
  67.4 0.1 eq.49
  67.5 1.3 convolution_convert_fusion.3
  68.8 0.2 reduce-scatter.5.cloned.1.call-start
  69.1 67.2 %all-gather.5.cloned.1.call-done = bf16[1280,2048]{1,0:T(8,128)(2,1)} async-done(((bf16[160,2048]{1,0:T(8,128)(2,1)}), bf16[1280,2048]{1,0:T(8,128)(2,1)}) %all-gather.5.cloned.1.call-update) | async-done | bytes 5242896 | tf_op jit(solution)/shard_map/cond/branch_1_fun/all_gather | solution.py:75
  136.3 16.9 %convolution_convert_fusion.2 = bf16[1280,2048]{1,0:T(8,128)(2,1)} fusion(bf16[1,1024,2048]{2,1,0:T(8,128)(2,1)} %get-tuple-element.45, bf16[1280,2048]{1,0:T(8,128)(2,1)} %all-gather.5.cloned.1.call-done, bf16[1,2048,1024]{2,1,0:T(8,128)(2,1)} %get-tuple-element.44), kind=kOutput, calls=%fused_computation.13 | convolution fusion | flops 10742661120 | bytes 18874368 | tf_op jit(solution)/shard_map/cond/branch_1_fun/dot_general | solution.py:79
  154.9 0.1 dynamic_slice.5
  155.0 62.3 %reduce-scatter.5.cloned.1.call-done = bf16[160,2048]{1,0:T(8,128)(2,1)} async-done(((bf16[1280,2048]{1,0:T(8,128)(2,1)}), bf16[160,2048]{1,0:T(8,128)(2,1)}) %reduce-scatter.5.cloned.1.call-update) | async-done | bytes 655376 | tf_op jit(solution)/shard_map/cond/branch_1_fun/reduce_scatter | solution.py:80
  217.3 1.6 fusion.13
  219.1 24.3 %all_to_all.10 = bf16[32,8,2048]{2,1,0:T(8,128)(2,1)S(1)} all-to-all(bf16[32,8,2048]{2,1,0:T(8,128)(2,1)S(1)} %bitcast.57), channel_id=1, replica_groups=mesh['dp'=8,'expert_0'=4,'expert_1'=4,'expert_2'=2] {'expert_0','expert_..., dimensions={0} | all-to-all | bytes 2097152 | tf_op jit(solution)/shard_map/all_to_all | solution.py:95
  243.4 1.5 fusion.18
  (25 shorter events, 0.2 us)
Async XLA Ops:
  6.5 2.0 copy-start
  6.5 42.4 %copy-start.1 = (f32[1,128]{1,0:T(1,128)S(1)}, f32[1,128]{1,0:T(1,128)}, u32[]{:S(2)}) copy-start(f32[1,128]{1,0:T(1,128)} %param.13) | copy-start | bytes 1540
  10.0 57.4 %all-to-all-start = ((bf16[32,8,2048]{2,1,0:T(8,128)(2,1)}), bf16[32,8,2048]{2,1,0:T(8,128)(2,1)S(1)}, u32[]{:S(2)}, u32[]{:S(2)}) async-start(bf16[32,8,2048]{2,1,0:T(8,128)(2,1)} %fusion.19), calls=%async_computation.2 | async-start | bytes 2097152 | tf_op jit(solution)/shard_map/all_to_all | solution.py:33
  67.4 68.9 %all-gather.5.cloned.1.call-start = ((), (), s32[]{:S(2)}) async-start(), calls=%async_computation.6 | async-start | bytes 5898240 | tf_op jit(solution)/shard_map/cond/branch_1_fun/all_gather | solution.py:75
  68.8 148.5 %reduce-scatter.5.cloned.1.call-start = ((), (), s32[]{:S(2)}) async-start(), calls=%async_computation.7 | async-start | bytes 5898240 | tf_op jit(solution)/shard_map/cond/branch_1_fun/reduce_scatter | solution.py:80
Sparse Core Ops, SparseCore 0:
  70.0 66.2 all-gather.4
  153.3 63.9 reduce-scatter.4

commit v2 on v0

--- a/solution.py
+++ b/solution.py
@@ -36,7 +36,11 @@
     device_ids = lax.broadcasted_iota(jnp.int32, (expert_count, expert_count), 0)
     expert_ids = lax.broadcasted_iota(jnp.int32, (expert_count, expert_count), 1)
     table = jnp.where(device_ids == own_expert, counts[None, :], 0)
-    table = lax.psum(table.reshape(-1, LANES), EXPERT).reshape(expert_count, expert_count)
+    table = (
+        lax.all_gather(table.reshape(-1, LANES), EXPERT)
+        .sum(axis=0)
+        .reshape(expert_count, expert_count)
+    )
     arrived = jnp.sum(jnp.where(expert_ids == own_expert, table, 0), axis=1)
     plane_ids = lax.broadcasted_iota(jnp.int32, (dp_count, LANES), 0)
     lane_ids = lax.broadcasted_iota(jnp.int32, (dp_count, LANES), 1)

time: 349 us -> 251 us (0.72)
  blocking collectives: 168 us -> 73 us
    psum x1 -> x0, blocking collectives: 127 us -> none  [on_device(): lax.psum(table.reshape(-1, LANES), EXPERT)]
    all_gather x0 -> x1, blocking collectives: none -> 32.2 us  [on_device(): lax.all_gather(table.reshape(-1, LANES), EXPERT).sum(axis=0)]
where the time goes in v2:
time: 251 us
  waiting for transfers between devices  126 us (50%)
  blocking collectives  73 us (29%)
  matrix products  22.7 us (9%)
  between operations  14.2 us (6%)
  starting transfers between devices  8.84 us (4%)
  other arithmetic  2.99 us (1%)
    all_gather x1, waiting for transfers between devices, experts(): slot_rows = lax.all_gather(plane, 'dp', axis=0, tiled=True)  64.1 us
    reduce_scatter x1, waiting for transfers between devices, experts(): lax.psum_scatter(share.astype(jnp.bfloat16), 'dp', scatter_dimension=0, t...  62.3 us
    all_gather x1, blocking collectives, on_device(): lax.all_gather(table.reshape(-1, LANES), EXPERT).sum(axis=0)  32.2 us
    all_to_all x1, blocking collectives, on_device(): lax.all_to_all(sent_back.reshape(expert_count, MOST, width), EXPERT, spli...  24.3 us
    dot_general x1, matrix products, experts(): share = jnp.dot(hidden, weight_out[0], preferred_element_type=jnp.float32)  16.9 us
    psum x1, blocking collectives, on_device(): both = lax.psum(both, 'dp')  16.5 us
    all_to_all x1, starting transfers between devices, on_device(): lax.all_to_all(packed.reshape(expert_count, MOST, width), EXPERT, split_a...  8.58 us
  transfers between devices with their start and end apart: 3, of which 2 were waited for; matrix products, arithmetic and copies ran while one was open for 1% of the time, Pallas kernels for 0%

profile of v2, /device:TPU:1, one launch (start us, length us, event | category | flops | bytes accessed | tf_op | source)
XLA Modules:
  0.0 250.9 jit_solution(1714099159479907801)
XLA Ops:
  6.5 0.9 convert_bitcast_fusion.1
  7.5 0.6 reduce-window.18
  8.1 0.2 slice_reduce_fusion
  8.3 0.1 iota.90
  8.4 0.1 convert_subtract_fusion
  8.5 1.5 fusion.19
  10.0 8.6 %all-to-all-start = ((bf16[32,8,2048]{2,1,0:T(8,128)(2,1)}), bf16[32,8,2048]{2,1,0:T(8,128)(2,1)S(1)}, u32[]{:S(2)}, u32[]{:S(2)}) async-start(bf16[32,8,2048]{2,1,0:T(8,128)(2,1)} %fusion.19), calls=%async_computation.2 | async-start | bytes 2097152 | tf_op jit(solution)/shard_map/all_to_all | solution.py:33
  18.6 0.1 iota.79
  18.7 0.1 iota.80
  18.8 0.1 broadcast_in_dim.59
  18.9 32.2 %all_gather.9 = s32[32,8,128]{2,1,0:T(8,128)S(1)} all-gather(s32[1,8,128]{2,1,0:T(8,128)S(1)} %broadcast_select_fusion.2), channel_id=1, replica_groups=mesh['dp'=8,'expert_0'=4,'expert_1'=4,'expert_2'=2] {'expert_0','expert_..., dimensions={0}, use_global_device_ids=true | all-gather | bytes 135168 | tf_op jit(solution)/shard_map/all_gather | solution.py:40
  51.1 0.1 reshape.104
  51.2 0.1 select_reduce_fusion
  51.3 0.1 broadcast_select_fusion.1
  51.4 16.5 %psum.7 = f32[16,128]{1,0:T(8,128)S(1)} all-reduce(f32[16,128]{1,0:T(8,128)S(1)} %pad_maximum_fusion), channel_id=1, replica_groups=mesh['dp'=8,'expert_0'=4,'expert_1'=4,'expert_2'=2] {'dp'}, use_global_device_ids=true, to_apply=%region_5.6 | all-reduce | flops 2048 | bytes 16384 | tf_op jit(solution)/shard_map/psum | solution.py:54
  67.9 0.8 select_reduce_fusion.1
  69.4 0.1 copy.19
  69.5 0.1 reduce-window.20
  69.5 0.1 reduce.1
  69.7 0.1 add_select_fusion
  69.8 148.6 %conditional.2 = (bf16[256,2048]{1,0:T(8,128)(2,1)S(1)}) conditional(s32[]{:T(128)} %convert_element_type.61, (s32[32,8]{1,0:T(8,128)S(1)}, s32[]{:T(128)}, f32[1280]{0:T(1024)S(1)}, bf16[256,2048]{1,0:T(8,128)(2,1)S(1)}, bf16[1,2048,1024]{2,1,0:T(8,128)(2,1)}, /*index=5*/bf16[1,1024,2048]{2,1,0:T(8,128)(2,1)}) %tuple.30, (s32[32,8]{1,0:T(8,128)S(1)}, ...), branch_computations={%region_10.12_spmd, %region_12.14_spmd} | conditional | flops 17727356928 | bytes 85990520
  69.8 0.0 all-gather.5.cloned.1.call-start
  69.8 0.1 eq.49
  69.9 1.3 convolution_convert_fusion.3
  71.3 0.2 reduce-scatter.5.cloned.1.call-start
  71.5 64.1 %all-gather.5.cloned.1.call-done = bf16[1280,2048]{1,0:T(8,128)(2,1)} async-done(((bf16[160,2048]{1,0:T(8,128)(2,1)}), bf16[1280,2048]{1,0:T(8,128)(2,1)}) %all-gather.5.cloned.1.call-update) | async-done | bytes 5242896 | tf_op jit(solution)/shard_map/cond/branch_1_fun/all_gather | solution.py:71
  135.5 16.9 %convolution_convert_fusion.2 = bf16[1280,2048]{1,0:T(8,128)(2,1)} fusion(bf16[1,1024,2048]{2,1,0:T(8,128)(2,1)} %get-tuple-element.45, bf16[1280,2048]{1,0:T(8,128)(2,1)} %all-gather.5.cloned.1.call-done, bf16[1,2048,1024]{2,1,0:T(8,128)(2,1)} %get-tuple-element.44), kind=kOutput, calls=%fused_computation.13 | convolution fusion | flops 10742661120 | bytes 18874368 | tf_op jit(solution)/shard_map/cond/branch_1_fun/dot_general | solution.py:75
  154.1 0.1 dynamic_slice.5
  154.2 62.3 %reduce-scatter.5.cloned.1.call-done = bf16[160,2048]{1,0:T(8,128)(2,1)} async-done(((bf16[1280,2048]{1,0:T(8,128)(2,1)}), bf16[160,2048]{1,0:T(8,128)(2,1)}) %reduce-scatter.5.cloned.1.call-update) | async-done | bytes 655376 | tf_op jit(solution)/shard_map/cond/branch_1_fun/reduce_scatter | solution.py:76
  216.5 1.6 fusion.13
  218.4 24.3 %all_to_all.10 = bf16[32,8,2048]{2,1,0:T(8,128)(2,1)S(1)} all-to-all(bf16[32,8,2048]{2,1,0:T(8,128)(2,1)S(1)} %bitcast.57), channel_id=1, replica_groups=mesh['dp'=8,'expert_0'=4,'expert_1'=4,'expert_2'=2] {'expert_0','expert_..., dimensions={0} | all-to-all | bytes 2097152 | tf_op jit(solution)/shard_map/all_to_all | solution.py:91
  242.6 1.5 fusion.18
  (25 shorter events, 0.2 us)
Async XLA Ops:
  6.5 2.0 copy-start
  6.5 44.8 %copy-start.1 = (f32[1,128]{1,0:T(1,128)S(1)}, f32[1,128]{1,0:T(1,128)}, u32[]{:S(2)}) copy-start(f32[1,128]{1,0:T(1,128)} %param.13) | copy-start | bytes 1540
  10.0 59.8 %all-to-all-start = ((bf16[32,8,2048]{2,1,0:T(8,128)(2,1)}), bf16[32,8,2048]{2,1,0:T(8,128)(2,1)S(1)}, u32[]{:S(2)}, u32[]{:S(2)}) async-start(bf16[32,8,2048]{2,1,0:T(8,128)(2,1)} %fusion.19), calls=%async_computation.2 | async-start | bytes 2097152 | tf_op jit(solution)/shard_map/all_to_all | solution.py:33
  69.8 65.7 %all-gather.5.cloned.1.call-start = ((), (), s32[]{:S(2)}) async-start(), calls=%async_computation.6 | async-start | bytes 5898240 | tf_op jit(solution)/shard_map/cond/branch_1_fun/all_gather | solution.py:71
  71.3 145.3 %reduce-scatter.5.cloned.1.call-start = ((), (), s32[]{:S(2)}) async-start(), calls=%async_computation.7 | async-start | bytes 5898240 | tf_op jit(solution)/shard_map/cond/branch_1_fun/reduce_scatter | solution.py:76
Sparse Core Ops, SparseCore 0:
  72.4 63.1 all-gather.4
  152.6 63.9 reduce-scatter.4
